TPU v7x, 128 devices: a whole 4x4x4 slice. The times are simulated.
128 devices in a mesh: seq: 16 (over y, x), head: 8 (over z, core).
Axes of the slice: x: 4, y: 4, z: 4, core: 2. Of those that a mesh axis runs over, the one named last changes fastest.
Arguments:
- segment_input: bfloat16 [2, 4096, 3584], P(None, 'seq'), may hold values from -16 to 16
- doc_ids: int32 [2, 4096], replicated, may hold values from 0 to 3, never falling along the last dimension, each value on 1 to 2048 neighbouring positions
- memory: bfloat16 [32, 3584], replicated, may hold values from -16 to 16
- gain: bfloat16 [3584], replicated, may hold values from 0.099609375 to 1.8984375
- w_query: bfloat16 [3584, 4096], P(None, 'head'), may hold values from -4 to 4
- w_key: bfloat16 [3584, 2048], P(None, 'head'), may hold values from -4 to 4
- w_value: bfloat16 [3584, 2048], P(None, 'head'), may hold values from -0.09375 to 0.09375
- w_out: bfloat16 [4096, 3584], P(None, 'head'), may hold values from -0.09375 to 0.09375
- mem_proj: bfloat16 [3584, 3584], P('head'), may hold values from -4 to 4
Outputs:
- hidden: bfloat16 [2, 4096, 3584], P(None, 'seq', 'head')
- new_memory: bfloat16 [32, 3584], replicated
Inputs may be any that keep to these rules, and one draw needn't show every extreme that they name: `doc_ids`: ids never fall along a segment; each document has 1 to 2048 tokens.
All inputs are finite; a program needn't handle non-finite values.
Results may differ from a plain program's by a relative error of at most 0.02.
Values may be sent and summed in bfloat16 or wider, within the bound.
No kernel may reach another device: no remote copies, remote signals or barrier semaphores. Data moves between devices by JAX's collectives and lax.ppermute only.
A program may use at most 128 MiB of HBM per device.

v0:
```python
import functools
import math

import jax
import jax.numpy as jnp
from jax import lax
from jax.experimental import pallas as pl
from jax.experimental.pallas import tpu as pltpu
from jax.sharding import PartitionSpec as P


D = 3584
HD = 256
M = 32
ROWS = 256
COLS = 448
HALF = D // 2
KC = 512
SHAPE = 4
LOG2E_SCALE = math.log2(math.e) / 16.0
LOW = -1e30
BF = jnp.bfloat16
F32 = jnp.float32


WHOLE = pl.BlockSpec(memory_space=pltpu.VMEM)


def params(mib, **kw):
    return pltpu.CompilerParams(vmem_limit_bytes=mib * 1024 * 1024, **kw)


def dot(a, b):
    return jnp.dot(a, b, preferred_element_type=F32)


def dot_t(a, b):
    return lax.dot_general(a, b, (((1,), (1,)), ((), ())), preferred_element_type=F32)


def normed(rows, gain):
    v = rows.astype(F32)
    r = lax.rsqrt(jnp.mean(v * v, axis=-1, keepdims=True) + 1e-6)
    return (v * r * gain.astype(F32)).astype(BF)


def column(row):
    return jnp.broadcast_to(row, (128, row.shape[1])).T[:, :1]


def as_row(col):
    return jnp.broadcast_to(col, (col.shape[0], 128)).T[:1, :]


def attend(score_list, value_list):
    peak = functools.reduce(jnp.maximum, [jnp.max(s, axis=1, keepdims=True) for s in score_list])
    peak = jnp.maximum(peak, -1e29)
    total = 0.0
    mixed = 0.0
    for s, v in zip(score_list, value_list):
        p = jnp.exp2(s - peak)
        total = total + jnp.sum(p, axis=1, keepdims=True)
        mixed = mixed + dot(p.astype(BF), v)
    some = total > 0.0
    out = mixed / jnp.where(some, total, 1.0)
    return out, jnp.where(some, peak + jnp.log2(jnp.where(some, total, 1.0)), LOW)


def memory_part(qkvm, key_blocks, first, out_ref):
    for g in range(2):
        q = qkvm[:, g * HD : (g + 1) * HD]
        scores = [dot_t(q, kv[:, :HD]) * LOG2E_SCALE for kv in key_blocks]
        sm = dot_t(q, qkvm[:, 2 * HD : 3 * HD]) * LOG2E_SCALE
        scores.append(jnp.where(first, sm, LOW))
        out, lse = attend(scores, [kv[:, HD:] for kv in key_blocks] + [qkvm[:, 3 * HD :]])
        hi = lse.astype(BF)
        lo = (lse - hi.astype(F32)).astype(BF)
        lane = lax.broadcasted_iota(jnp.int32, (M, 128), 1)
        stats = jnp.where(lane == 0, hi.astype(F32), jnp.where(lane == 1, lo.astype(F32), 0.0))
        out_ref[g * M : (g + 1) * M, :HD] = out.astype(BF)
        out_ref[g * M : (g + 1) * M, HD:] = stats.astype(BF)


def place():
    i = lax.axis_index("seq")
    h = lax.axis_index("head")
    return i % SHAPE, i // SHAPE, h // 2, h % 2


def scaled_chunk(x, gain, squares, rows, first):
    v = x.astype(F32)
    sq = v * v
    part = sq[:, :128]
    for n in range(1, KC // 128):
        part = part + sq[:, n * 128 : (n + 1) * 128]
    squares[rows, :] = part if first else squares[rows, :] + part
    return (v * gain).astype(BF)


def norm_of(squares):
    return lax.rsqrt(jnp.sum(squares[...], axis=1, keepdims=True) / D + 1e-6)


def accumulate(acc, a, ws, first):
    at = 0
    for w in ws:
        span = slice(at, at + w.shape[1])
        part = dot(a, w)
        acc[:, span] = part if first else acc[:, span] + part
        at = at + w.shape[1]


def first_kernel(x, mem, gain, wq, wk, wv, q_ref, kv_ref, qkvm_ref, part_ref, *refs):
    bufs, (xs, ms, squares, acc, sems) = refs[:3], refs[3:]
    groups = []
    for k in range(D // KC):
        span = pl.ds(k * KC, KC)
        pairs = [(x.at[0, :, span], xs.at[:, span]), (mem.at[:, span], ms.at[:, span])]
        pairs += [(w.at[span, :], buf.at[span, :]) for w, buf in zip((wq, wk, wv), bufs)]
        groups.append(
            [pltpu.make_async_copy(p, q, sems.at[k, n]) for n, (p, q) in enumerate(pairs)]
        )
    for group in groups:
        for c in group:
            c.start()
    g = gain[...].astype(F32).reshape(1, D)
    for k, group in enumerate(groups):
        for c in group:
            c.wait()
        span = slice(k * KC, (k + 1) * KC)
        top = scaled_chunk(xs[:, span], g[:, span], squares, slice(0, ROWS), k == 0)
        low = scaled_chunk(ms[:, span], g[:, span], squares, slice(ROWS, ROWS + M), k == 0)
        a = jnp.concatenate([top, low], axis=0)
        accumulate(acc, a, [buf[span, :] for buf in bufs], k == 0)
    out = (acc[...] * norm_of(squares)).astype(BF)
    q_ref[...] = out[:ROWS, : 2 * HD]
    kv_ref[...] = out[:ROWS, 2 * HD :]
    qkvm_ref[...] = out[ROWS:, :]
    px, py, _, _ = place()
    memory_part(qkvm_ref[...], [kv_ref[...]], px + py == 0, part_ref)


def first_project(x, mem, gain, wq, wk, wv):
    hbm = pl.BlockSpec(memory_space=pltpu.HBM)
    shapes = [(ROWS, 2 * HD), (ROWS, 2 * HD), (M, 4 * HD), (2 * M, HD + 128)]
    shapes += [wq.shape, wk.shape, wv.shape]
    return pl.pallas_call(
        first_kernel,
        in_specs=[hbm, hbm, WHOLE, hbm, hbm, hbm],
        out_specs=[WHOLE] * len(shapes),
        out_shape=[jax.ShapeDtypeStruct(s, BF) for s in shapes],
        scratch_shapes=[
            pltpu.VMEM((ROWS, D), BF),
            pltpu.VMEM((M, D), BF),
            pltpu.VMEM((ROWS + M, 128), F32),
            pltpu.VMEM((ROWS + M, 4 * HD), F32),
            pltpu.SemaphoreType.DMA((D // KC, 5)),
        ],
        compiler_params=params(28),
        cost_estimate=pl.CostEstimate(
            flops=2 * (ROWS + M) * D * 4 * HD, bytes_accessed=10 * 2**20, transcendentals=512
        ),
        name="first_project",
    )(x, mem, gain, wq, wk, wv)


def window(h):
    return pl.multiple_of((h * 7 // 2) * 128, 128)


def second_kernel(x, gain, wq, wk, wv, wt, proj, *refs):
    q_ref, kv_ref, wt_buf, proj_buf, cols_buf, xs, squares, acc, sems, wsems = refs
    _, _, z, c = place()
    copies = []
    for k in range(D // KC):
        span = pl.ds(k * KC, KC)
        copies.append(pltpu.make_async_copy(x.at[1, :, span], xs.at[:, span], sems.at[k]))
    late = [
        pltpu.make_async_copy(src, dst, wsems.at[n])
        for n, (src, dst) in enumerate(
            (
                (wt, wt_buf),
                (proj, proj_buf),
                (x.at[:, :, pl.ds(window(2 * z + c), 512)], cols_buf),
            )
        )
    ]
    for c in copies + late:
        c.start()
    g = gain[...].astype(F32).reshape(1, D)
    for k, c in enumerate(copies):
        c.wait()
        span = slice(k * KC, (k + 1) * KC)
        a = scaled_chunk(xs[:, span], g[:, span], squares, slice(0, ROWS), k == 0)
        accumulate(acc, a, [w[span, :] for w in (wq, wk, wv)], k == 0)
    out = (acc[...] * norm_of(squares)).astype(BF)
    q_ref[...] = out[:, : 2 * HD]
    kv_ref[...] = out[:, 2 * HD :]
    for c in late:
        c.wait()


def second_project(x, gain, wq, wk, wv, wt, proj):
    hbm = pl.BlockSpec(memory_space=pltpu.HBM)
    shapes = [(ROWS, 2 * HD), (ROWS, 2 * HD), wt.shape, proj.shape, (2, ROWS, 512)]
    return pl.pallas_call(
        second_kernel,
        in_specs=[hbm] + [WHOLE] * 4 + [hbm, hbm],
        out_specs=[WHOLE] * len(shapes),
        out_shape=[jax.ShapeDtypeStruct(s, BF) for s in shapes],
        scratch_shapes=[
            pltpu.VMEM((ROWS, D), BF),
            pltpu.VMEM((ROWS, 128), F32),
            pltpu.VMEM((ROWS, 4 * HD), F32),
            pltpu.SemaphoreType.DMA((D // KC,)),
            pltpu.SemaphoreType.DMA((3,)),
        ],
        compiler_params=params(28),
        cost_estimate=pl.CostEstimate(
            flops=2 * ROWS * D * 4 * HD, bytes_accessed=10 * 2**20, transcendentals=512
        ),
        name="second_project",
    )(x, gain, wq, wk, wv, wt, proj)


def memory_project_kernel(own, other, gain, wq, wk, wv, *refs):
    kvs, (qkvm_ref, part_ref, whole_ref) = refs[:4], refs[4:]
    px, _, _, c = place()
    whole_ref[:, pl.ds(pl.multiple_of(c * HALF, 128), HALF)] = own[...]
    whole_ref[:, pl.ds(pl.multiple_of((1 - c) * HALF, 128), HALF)] = other[...]
    a = normed(whole_ref[...], gain[...].reshape(1, D))
    qkvm_ref[:, : 2 * HD] = dot(a, wq[...]).astype(BF)
    qkvm_ref[:, 2 * HD : 3 * HD] = dot(a, wk[...]).astype(BF)
    qkvm_ref[:, 3 * HD :] = dot(a, wv[...]).astype(BF)
    memory_part(qkvm_ref[...], [kv[...] for kv in kvs], px == 0, part_ref)


def memory_project(own, other, gain, wq, wk, wv, kvs):
    return pl.pallas_call(
        memory_project_kernel,
        in_specs=[WHOLE] * 10,
        out_specs=[WHOLE] * 3,
        out_shape=[
            jax.ShapeDtypeStruct((M, 4 * HD), BF),
            jax.ShapeDtypeStruct((2 * M, HD + 128), BF),
            jax.ShapeDtypeStruct((M, D), BF),
        ],
        compiler_params=params(20),
        cost_estimate=pl.CostEstimate(
            flops=2 * 256 * D * 4 * HD, bytes_accessed=8 * 1024 * 1024, transcendentals=M
        ),
        name="memory_project",
    )(own, other, gain, wq, wk, wv, *kvs)


def memory_combine_kernel(last, a, b, out_ref):
    parts = [r[...].astype(F32) for r in (a, b)]
    lses = [p[:, HD : HD + 1] + p[:, HD + 1 : HD + 2] for p in parts]
    peak = functools.reduce(jnp.maximum, lses)
    ws = [jnp.exp2(s - peak) for s in lses]
    total = sum(ws)
    out = sum(w * p[:, :HD] for w, p in zip(ws, parts)) / total
    if last:
        out_ref[:, :HD] = out[:M].astype(BF)
        out_ref[:, HD:] = out[M:].astype(BF)
    else:
        lse = peak + jnp.log2(total)
        hi = lse.astype(BF).astype(F32)
        lane = lax.broadcasted_iota(jnp.int32, (2 * M, 128), 1)
        stats = jnp.where(lane == 0, hi, jnp.where(lane == 1, lse - hi, 0.0))
        out_ref[:, :HD] = out.astype(BF)
        out_ref[:, HD:] = stats.astype(BF)


def memory_combine(a, b, last=False):
    shape = (M, 2 * HD) if last else (2 * M, HD + 128)
    return pl.pallas_call(
        functools.partial(memory_combine_kernel, last),
        in_specs=[WHOLE] * 2,
        out_specs=WHOLE,
        out_shape=jax.ShapeDtypeStruct(shape, BF),
        compiler_params=params(4),
        cost_estimate=pl.CostEstimate(flops=10**8, bytes_accessed=10**5, transcendentals=256),
        name="memory_combine",
    )(a, b)


def pair_kernel(a, b, out_ref):
    out_ref[0] = a[...]
    out_ref[1] = b[...]


def pair_up(a, b):
    return pl.pallas_call(
        pair_kernel,
        in_specs=[WHOLE] * 2,
        out_specs=WHOLE,
        out_shape=jax.ShapeDtypeStruct((2, *a.shape), BF),
        compiler_params=params(4),
        name="pair_up",
    )(a, b)


def first_kernel_of(v, out_ref):
    out_ref[...] = v[0]


def first_of(v):
    return pl.pallas_call(
        first_kernel_of,
        in_specs=[WHOLE],
        out_specs=WHOLE,
        out_shape=jax.ShapeDtypeStruct(v.shape[1:], BF),
        compiler_params=params(4),
        name="first_of",
    )(v)


def gathered_heads():
    _, _, z, c = place()
    side = 1 - 2 * c
    before, after = lax.rem(z - side + SHAPE, SHAPE), lax.rem(z + side + SHAPE, SHAPE)
    far = lax.rem(z + 2, SHAPE)
    chips = (z, z, before, before, after, after, far, far)
    cores = (c, 1 - c, c, 1 - c, 1 - c, c, c, 1 - c)
    return [2 * zz + cc for zz, cc in zip(chips, cores)]


def block_values(refs):
    own, swapped, near, near2, far, far2 = refs
    return [own[...], swapped[...], near[0], near[1], near2[0], near2[1], far[...], far2[...]]


def memory_write_kernel(o, o2, n, n2, f, f2, mem, w_out, proj, keep_ref, send_ref):
    _, _, z, c = place()
    wide = mem[:, pl.ds(window(2 * z + c), 512)].astype(F32)
    acc = jnp.where(c == 1, wide[:, 64:], wide[:, :COLS])
    for h, v in zip(gathered_heads(), block_values((o, o2, n, n2, f, f2))):
        acc = acc + dot_t(v, w_out[:, pl.ds(pl.multiple_of(h * 2 * HD, 2 * HD), 2 * HD)])
    a = acc.astype(BF)
    keep_ref[...] = dot(a, proj[:, pl.ds(pl.multiple_of(c * HALF, 128), HALF)]).astype(BF)
    send_ref[...] = dot(a, proj[:, pl.ds(pl.multiple_of((1 - c) * HALF, 128), HALF)]).astype(BF)


def finish_kernel(own, other, out_ref):
    _, _, _, c = place()
    out_ref[:, pl.ds(pl.multiple_of(c * HALF, 128), HALF)] = own[...]
    out_ref[:, pl.ds(pl.multiple_of((1 - c) * HALF, 128), HALF)] = other[...]


def finish(own, other):
    return pl.pallas_call(
        finish_kernel,
        in_specs=[WHOLE] * 2,
        out_specs=WHOLE,
        out_shape=jax.ShapeDtypeStruct((M, D), BF),
        compiler_params=params(4),
        name="finish",
    )(own, other)


def memory_write(blocks, mem, w_out, proj):
    return pl.pallas_call(
        memory_write_kernel,
        in_specs=[WHOLE] * 9,
        out_specs=[WHOLE] * 2,
        out_shape=[jax.ShapeDtypeStruct((M, HALF), BF)] * 2,
        compiler_params=params(20),
        cost_estimate=pl.CostEstimate(
            flops=2 * 256 * D * 8 * COLS, bytes_accessed=8 * 1024 * 1024, transcendentals=0
        ),
        name="memory_write",
    )(*blocks, mem, w_out, proj)


def stack_kernel(kva, kvb, kvb2, kvc, kvs, send):
    x, y, _, _ = place()
    kvs[:ROWS, :] = kva[...]
    kvs[ROWS : 2 * ROWS, :] = jnp.where(y % 2 == 1, kvb[...], kvb2[...])
    kvs[2 * ROWS :, :] = kvc[...]
    at = pl.multiple_of(jnp.where(x >= 2, 0, ROWS), ROWS)
    send[...] = kvs[pl.ds(at, 2 * ROWS), :]


def stack(kva, kvb, kvb2, kvc):
    return pl.pallas_call(
        stack_kernel,
        in_specs=[WHOLE] * 4,
        out_specs=[WHOLE] * 2,
        out_shape=[
            jax.ShapeDtypeStruct((3 * ROWS, 2 * HD), BF),
            jax.ShapeDtypeStruct((2 * ROWS, 2 * HD), BF),
        ],
        compiler_params=params(8),
        name="stack",
    )(kva, kvb, kvb2, kvc)


def token_kernel(seg, docs, q0, q1, kvs, far_kvs, o0, o1, kcode):
    x, y, _, _ = place()
    lane = lax.broadcasted_iota(jnp.int32, (1, ROWS), 1).astype(F32)

    def codes_of(block):
        start = jnp.maximum(block, 0) * ROWS
        doc = docs[seg : seg + 1, pl.ds(pl.multiple_of(start, ROWS), ROWS)].astype(F32)
        return doc * 4096.0, doc * 4096.0 + lane + start.astype(F32)

    first_row = jnp.where(x >= 2, y - 1, y - 2)
    blocks = [(y - 2 + n) * SHAPE + x for n in range(3)]
    blocks += [(first_row + n) * SHAPE + (SHAPE - 1 - x) for n in range(2)]
    for n, block in enumerate(blocks):
        code = codes_of(block)[1]
        kcode[:, n * ROWS : (n + 1) * ROWS] = jnp.where(block >= 0, code, -1.0)
    near = lax.bitwise_xor(x, 1)
    for e, (q_ref, o_ref) in enumerate(((q0, o0), (q1, o1))):
        low, high = codes_of(y * SHAPE + (x if e == 0 else near))
        low, high = column(low), column(high)
        if e == 0:
            span = slice(0, 3 * ROWS)
        else:
            span = pl.ds(pl.multiple_of(jnp.where(near < x, 0, ROWS), ROWS), 2 * ROWS)
        keys = [kvs[span, :], far_kvs[...]]
        codes = [kcode[:, span], kcode[:, 3 * ROWS :]]
        valid = [(k >= low) & (k <= high) for k in codes]
        for g in range(2):
            q = q_ref[:, g * HD : (g + 1) * HD]
            scores = [
                jnp.where(v, dot_t(q, k[:, :HD]) * LOG2E_SCALE, LOW) for v, k in zip(valid, keys)
            ]
            out, lse = attend(scores, [k[:, HD:] for k in keys])
            row = as_row(lse)
            hi = row.astype(BF).astype(F32)
            sub = lax.broadcasted_iota(jnp.int32, (16, ROWS), 0)
            stats = jnp.where(sub == 0, hi, jnp.where(sub == 1, row - hi, 0.0))
            o_ref[:ROWS, g * HD : (g + 1) * HD] = out.astype(BF)
            o_ref[ROWS:, g * HD : (g + 1) * HD] = stats.astype(BF)


def token_attention(docs, seg, q, near_q, kvs, far_kvs):
    return pl.pallas_call(
        functools.partial(token_kernel, seg),
        in_specs=[WHOLE] * 5,
        out_specs=[WHOLE] * 2,
        out_shape=[jax.ShapeDtypeStruct((ROWS + 16, 2 * HD), BF)] * 2,
        scratch_shapes=[pltpu.VMEM((1, 5 * ROWS), F32)],
        compiler_params=params(16),
        cost_estimate=pl.CostEstimate(
            flops=3 * 10**9, bytes_accessed=4 * 10**6, transcendentals=10**6
        ),
        name="token_attention",
    )(docs, q, near_q, kvs, far_kvs)


def token_combine_kernel(q, qkvm, a, b, out_ref):
    refs = (a, b)
    for g in range(2):
        lanes = slice(g * HD, (g + 1) * HD)
        scores = dot_t(q[:, lanes], qkvm[:, 2 * HD : 3 * HD]) * LOG2E_SCALE
        out, lse = attend([scores], [qkvm[:, 3 * HD :]])
        outs, lses = [out], [lse]
        for r in refs:
            tail = r[ROWS:, lanes].astype(F32)
            lses.append(column(tail[0:1, :] + tail[1:2, :]))
            outs.append(r[:ROWS, lanes].astype(F32))
        peak = functools.reduce(jnp.maximum, lses)
        ws = [jnp.exp2(s - peak) for s in lses]
        mixed = sum(w * o for w, o in zip(ws, outs)) / sum(ws)
        out_ref[:, lanes] = mixed.astype(BF)


def token_combine(q, qkvm, parts):
    return pl.pallas_call(
        token_combine_kernel,
        in_specs=[WHOLE] * 4,
        out_specs=WHOLE,
        out_shape=jax.ShapeDtypeStruct((ROWS, 2 * HD), BF),
        compiler_params=params(12),
        cost_estimate=pl.CostEstimate(flops=5 * 10**8, bytes_accessed=10**6, transcendentals=4096),
        name="token_combine",
    )(q, qkvm, *parts)


def token_out_kernel(seg, *refs):
    blocks, cols, w_out, out_ref, flat = refs[:6], *refs[6:]
    acc = features(cols, seg, flat)
    for h, v in zip(gathered_heads(), block_values(blocks)):
        acc = acc + dot_t(w_out[:, pl.ds(pl.multiple_of(h * 2 * HD, 2 * HD), 2 * HD)], v)
    out_ref[0] = acc.astype(BF)


def features(cols, seg, flat):
    _, _, _, c = place()
    for at in range(0, 512, 128):
        flat[at : at + 128, :] = cols[seg, :, at : at + 128].astype(F32).T
    return flat[pl.ds(pl.multiple_of(c * 64, 64), COLS), :]


def token_out(blocks, cols, seg, w_out):
    return pl.pallas_call(
        functools.partial(token_out_kernel, seg),
        grid=(1,),
        in_specs=[WHOLE] * 8,
        out_specs=pl.BlockSpec((1, COLS, ROWS), lambda k: (seg, 0, 0)),
        out_shape=jax.ShapeDtypeStruct((2, COLS, ROWS), BF),
        scratch_shapes=[pltpu.VMEM((512, ROWS), F32)],
        compiler_params=params(12),
        cost_estimate=pl.CostEstimate(
            flops=2 * ROWS * 4096 * COLS, bytes_accessed=6 * 10**6, transcendentals=0
        ),
        name="token_out",
    )(*blocks, cols, w_out)


def early_kernel(seg, *refs):
    cols, w_out, out_ref, flat = refs[4:]
    own, swapped, near, near2 = refs[:4]
    values = [own[...], swapped[...], near[0], near[1], near2[0], near2[1]]
    acc = features(cols, seg, flat)
    for h, v in zip(gathered_heads(), values):
        acc = acc + dot_t(w_out[:, pl.ds(pl.multiple_of(h * 2 * HD, 2 * HD), 2 * HD)], v)
    out_ref[...] = acc


def token_out_early(blocks, cols, seg, w_out):
    return pl.pallas_call(
        functools.partial(early_kernel, seg),
        in_specs=[WHOLE] * 6,
        out_specs=WHOLE,
        out_shape=jax.ShapeDtypeStruct((COLS, ROWS), F32),
        scratch_shapes=[pltpu.VMEM((512, ROWS), F32)],
        compiler_params=params(12),
        cost_estimate=pl.CostEstimate(
            flops=2 * ROWS * 3072 * COLS, bytes_accessed=5 * 10**6, transcendentals=0
        ),
        name="token_out_early",
    )(*blocks, cols, w_out)


def late_kernel(far, far2, early, w_out, before, out_ref):
    acc = early[...]
    for h, v in zip(gathered_heads()[6:], (far[...], far2[...])):
        acc = acc + dot_t(w_out[:, pl.ds(pl.multiple_of(h * 2 * HD, 2 * HD), 2 * HD)], v)
    out_ref[0] = acc.astype(BF)


def token_out_late(far, far2, early, seg, w_out, before):
    return pl.pallas_call(
        late_kernel,
        grid=(1,),
        in_specs=[WHOLE] * 4 + [pl.BlockSpec(memory_space=pl.ANY)],
        out_specs=pl.BlockSpec((1, COLS, ROWS), lambda k: (seg, 0, 0)),
        out_shape=jax.ShapeDtypeStruct((2, COLS, ROWS), BF),
        input_output_aliases={4: 0},
        compiler_params=params(12),
        cost_estimate=pl.CostEstimate(
            flops=2 * ROWS * 1024 * COLS, bytes_accessed=3 * 10**6, transcendentals=0
        ),
        name="token_out_late",
    )(far, far2, early, w_out, before)


N_SEQ, N_HEAD = SHAPE * SHAPE, 8


def x_xor(v, d):
    return lax.ppermute(v, "seq", [(i, i ^ d) for i in range(N_SEQ)])


def y_xor(v, d):
    return x_xor(v, 4 * d)


def y_later(v):
    return lax.ppermute(v, "seq", [(i, i + SHAPE) for i in range(N_SEQ - SHAPE)])


def all_four(send, v):
    near = send(v, 1)
    return [v, near, send(near, 3), send(v, 3)]


def x_near(v):
    return lax.ppermute(v, "seq", [(i, i ^ 1) for i in range(N_SEQ)])


def x_far(v):
    return lax.ppermute(v, "seq", [(i, i ^ 3) for i in range(N_SEQ)])


def y_near(v):
    return lax.ppermute(v, "seq", [(i, i ^ 4) for i in range(N_SEQ)])


def y_far(v):
    return lax.ppermute(v, "seq", [(i, i ^ 12) for i in range(N_SEQ)])


def z_xor(v, d):
    return lax.ppermute(v, "head", [(i, i ^ (2 * d)) for i in range(N_HEAD)])


def z_turn(v):
    return lax.ppermute(v, "head", [(i, (i + 2 - 4 * (i % 2)) % N_HEAD) for i in range(N_HEAD)])


def other_core(v):
    return lax.ppermute(v, "head", [(i, i ^ 1) for i in range(N_HEAD)])


def add(a, b):
    return (a.astype(F32) + b.astype(F32)).astype(BF)


def gather_heads_direct(v):
    far = z_xor(v, 2)
    swapped = other_core(v)
    near = z_turn(pair_up(v, swapped))
    near2 = other_core(near)
    return v, swapped, near, near2, far, other_core(far)


def gather_heads(v):
    swapped = other_core(v)
    near = z_turn(pair_up(v, swapped))
    far = z_turn(first_of(near))
    near2 = other_core(near)
    return v, swapped, near, near2, far, other_core(far)


def memory_tail(attn, mem, w_out, proj):
    blocks = gather_heads_direct(attn)
    keep, send = memory_write(blocks, mem, w_out, proj)
    half = add(keep, other_core(send))
    near, far, two = [z_xor(half, d) for d in (1, 3, 2)]
    half = ((half.astype(F32) + near.astype(F32)) + (far.astype(F32) + two.astype(F32))).astype(BF)
    return half, other_core(half)


def per_device(segment_input, doc_ids, memory, gain, w_query, w_key, w_value, w_out, mem_proj):
    in_hbm = lambda v: pltpu.with_memory_space_constraint(v, pltpu.HBM)
    x = in_hbm(segment_input)

    q0, kv0, qkvm0, part, *weights = first_project(
        x, in_hbm(memory), gain, *[in_hbm(w) for w in (w_query, w_key, w_value)]
    )
    weights = (gain, *weights)
    q1, kv1, w_out, mem_proj, cols = second_project(x, *weights, in_hbm(w_out.T), in_hbm(mem_proj))

    part = memory_combine(part, x_near(part))
    part = memory_combine(part, x_far(part))
    part = memory_combine(part, y_near(part))
    attn = memory_combine(part, y_far(part), True)
    own, other = memory_tail(attn, memory, w_out, mem_proj)

    next_row = y_later(kv0)
    kvs0 = [kv0, next_row, y_later(next_row), next_row]
    kvs1 = all_four(y_xor, kv1)
    qkvm1, part, mem1 = memory_project(own, other, *weights, kvs1)
    part = memory_combine(part, x_near(part))
    attn = memory_combine(part, x_far(part), True)
    own, other = memory_tail(attn, mem1, w_out, mem_proj)

    for s, (kvs, qkvm) in enumerate(((kvs0, qkvm0), (kvs1, qkvm1))):
        own_q = (q0, q1)[s]
        near_q = x_xor(own_q, 1)
        stacked, send = stack(kvs[2], kvs[1], kvs[-1], kvs[0])
        far_kvs = x_xor(send, 3)
        mine, send = token_attention(doc_ids, s, own_q, near_q, stacked, far_kvs)
        parts = [mine, x_xor(send, 1)]
        attn = token_combine(own_q, qkvm, parts)
        blocks = gather_heads(attn)
        if s == 0:
            hidden = token_out(blocks, cols, s, w_out)
        else:
            early = token_out_early(blocks[:4], cols, s, w_out)
            hidden = token_out_late(*blocks[4:], early, s, w_out, hidden)
    return hidden.transpose(0, 2, 1), finish(own, other)


def solution(mesh):
    return jax.shard_map(
        per_device,
        mesh=mesh,
        in_specs=(
            P(None, "seq", None),
            P(),
            P(),
            P(),
            P(None, "head"),
            P(None, "head"),
            P(None, "head"),
            P(None, "head"),
            P("head", None),
        ),
        out_specs=(P(None, "seq", "head"), P()),
        check_vma=False,
    )
```

profile of v0, /device:TPU:23, one launch (start us, length us, event | category | flops | bytes accessed | tf_op | source)
XLA Modules:
  0.0 153.4 jit_solution(3922267564454926978)
XLA Ops:
  1.3 5.1 %first_project.1 = (bf16[256,512]{1,0:T(8,128)(2,1)S(1)}, bf16[256,512]{1,0:T(8,128)(2,1)S(1)}, bf16[32,1024]{1,0:T(8,128)(2,1)S(1)}, bf16[64,384]{1,0:T(8,128)(...) custom-call(bf16[2,256,3584]{2,1,0:T(8,128)(2,1)} %x.3, ...), custom_call_target="tpu_custom_call" | custom-call | flops 2113929216 | bytes 10485760 | tf_op jit(solution)/shard_map/first_project/pallas_call | solution.py:147
  9.9 4.0 %collective-permute-done.1.b = bf16[64,384]{1,0:T(8,128)(2,1)S(1)} collective-permute-done((bf16[64,384]{1,0:T(8,128)(2,1)S(1)}, bf16[64,384]{1,0:T(8,128)(2,1)S(1)}, u32[]{:S(2)}, u32[]{:S(2)}) %collective-permute-start.1) | collective-permute-done | bytes 49184 | tf_op jit(solution)/shard_map/ppermute | solution.py:587
  17.5 3.1 %collective-permute-done.3.b = bf16[64,384]{1,0:T(8,128)(2,1)S(1)} collective-permute-done((bf16[64,384]{1,0:T(8,128)(2,1)S(1)}, bf16[64,384]{1,0:T(8,128)(2,1)S(1)}, u32[]{:S(2)}, u32[]{:S(2)}) %collective-permute-start.3) | collective-permute-done | bytes 49184 | tf_op jit(solution)/shard_map/ppermute | solution.py:595
  20.8 5.1 %collective-permute-start.4 = (bf16[32,512]{1,0:T(8,128)(2,1)S(1)}, bf16[32,512]{1,0:T(8,128)(2,1)S(1)}, u32[]{:S(2)}, u32[]{:S(2)}) collective-permute-start(bf16[32,512]{1,0:T(8,128)(2,1)S(1)} %memory_combine.9.a.o), channel_id=1, source_target_pairs={{0,1},{1,0},{2,3},{3,2},{4,5},{5,4},{6,7},{7,6},{8,9},{9,8},{10,11... | collective-permute-start | bytes 98312 | tf_op jit(solution)/shard_map/ppermute | solution.py:607
  26.7 3.8 %collective-permute-start.5 = (bf16[2,32,512]{2,1,0:T(8,128)(2,1)S(1)}, bf16[2,32,512]{2,1,0:T(8,128)(2,1)S(1)}, u32[]{:S(2)}, u32[]{:S(2)}) collective-permute-start(bf16[2,32,512]{2,1,0:T(8,128)(2,1)S(1)} %pair_up.4), channel_id=1, source_target_pairs={{0,2},{1,7},{2,4},{3,1},{4,6},{5,3},{6,0},{7,5},{8,10},{9,15},{10,... | collective-permute-start | bytes 196616 | tf_op jit(solution)/shard_map/ppermute | solution.py:603
  30.5 4.4 %collective-permute-done.7.f = bf16[32,512]{1,0:T(8,128)(2,1)S(1)} collective-permute-done((bf16[32,512]{1,0:T(8,128)(2,1)S(1)}, bf16[32,512]{1,0:T(8,128)(2,1)S(1)}, u32[]{:S(2)}, u32[]{:S(2)}) %collective-permute-start.7) | collective-permute-done | bytes 32800 | tf_op jit(solution)/shard_map/ppermute | solution.py:599
  35.3 4.0 %second_project.1 = (bf16[256,512]{1,0:T(8,128)(2,1)S(1)}, bf16[256,512]{1,0:T(8,128)(2,1)S(1)}, bf16[448,4096]{1,0:T(8,128)(2,1)S(1)}, bf16[448,3584]{1,0:T(8,128)(2,1)S(1)}, bf16[2,256,512]{2,1,0:T(8,128)(2,1)S(1)}) custom-call(bf16[2,256,3584]{2,1,0:T(8,128)(2,1)} %x.3, bf16[3584]{0:T(1024)(128)(2,1)S(1)} %copy-done.1, ...), custom_call_target="tpu_custom_call" | custom-call | flops 1879048192 | bytes 10485760 | tf_op jit(solution)/shard_map/second_project/pallas_call | solution.py:206
  48.0 4.5 %collective-permute-done.26.kvb.kvb2 = bf16[256,512]{1,0:T(8,128)(2,1)S(1)} collective-permute-done((bf16[256,512]{1,0:T(8,128)(2,1)S(1)}, bf16[256,512]{1,0:T(8,128)(2,1)S(1)}, u32[]{:S(2)}, u32[]{:S(2)}) %collective-permute-start.26) | collective-permute-done | bytes 262176 | tf_op jit(solution)/shard_map/ppermute | solution.py:574
  52.6 4.1 %collective-permute-start.27 = (bf16[256,512]{1,0:T(8,128)(2,1)S(1)}, bf16[256,512]{1,0:T(8,128)(2,1)S(1)}, u32[]{:S(2)}, u32[]{:S(2)}) collective-permute-start(bf16[256,512]{1,0:T(8,128)(2,1)S(1)} %collective-permute-done.26.kvb.kvb2), channel_id=1, source_target_pairs={{0,32},{8,40},{16,48},{24,56},{32,64},{40,72},{48,80},{56,88},{64,... | collective-permute-start | bytes 786440 | tf_op jit(solution)/shard_map/ppermute | solution.py:574
  59.4 8.3 %collective-permute-done.27.kva = bf16[256,512]{1,0:T(8,128)(2,1)S(1)} collective-permute-done((bf16[256,512]{1,0:T(8,128)(2,1)S(1)}, bf16[256,512]{1,0:T(8,128)(2,1)S(1)}, u32[]{:S(2)}, u32[]{:S(2)}) %collective-permute-start.27) | collective-permute-done | bytes 262176 | tf_op jit(solution)/shard_map/ppermute | solution.py:574
  71.9 2.5 %collective-permute-start.18 = (bf16[512,512]{1,0:T(8,128)(2,1)S(1)}, bf16[512,512]{1,0:T(8,128)(2,1)S(1)}, u32[]{:S(2)}, u32[]{:S(2)}) collective-permute-start(bf16[512,512]{1,0:T(8,128)(2,1)S(1)} %get-tuple-element.41), channel_id=1, source_target_pairs={{0,24},{8,16},{16,8},{24,0},{32,56},{40,48},{48,40},{56,32},{64,88... | collective-permute-start | bytes 1572872 | tf_op jit(solution)/shard_map/ppermute | solution.py:566
  74.5 3.3 %collective-permute-start.13 = (bf16[32,1792]{1,0:T(8,128)(2,1)S(1)}, bf16[32,1792]{1,0:T(8,128)(2,1)S(1)}, u32[]{:S(2)}, u32[]{:S(2)}) collective-permute-start(bf16[32,1792]{1,0:T(8,128)(2,1)S(1)} %add_convert_fusion.2.own), channel_id=1, source_target_pairs={{0,1},{1,0},{2,3},{3,2},{4,5},{5,4},{6,7},{7,6},{8,9},{9,8},{10,11... | collective-permute-start | bytes 344072 | tf_op jit(solution)/shard_map/ppermute | solution.py:607
  77.8 5.1 %collective-permute-done.28.far_kvs = bf16[512,512]{1,0:T(8,128)(2,1)S(1)} collective-permute-done((bf16[512,512]{1,0:T(8,128)(2,1)S(1)}, bf16[512,512]{1,0:T(8,128)(2,1)S(1)}, u32[]{:S(2)}, u32[]{:S(2)}) %collective-permute-start.28) | collective-permute-done | bytes 524320 | tf_op jit(solution)/shard_map/ppermute | solution.py:566
  82.8 2.9 %token_attention.3 = (bf16[272,512]{1,0:T(8,128)(2,1)S(1)}, bf16[272,512]{1,0:T(8,128)(2,1)S(1)}) custom-call(s32[2,4096]{1,0:T(2,128)S(1)} %copy-done.3, bf16[256,512]{1,0:T(8,128)(2,1)S(1)} %get-tuple-element.45.q0.q, bf16[256,512]{1,0:T(8,128)(2,1)S(1)} %collective-permute-done.25.q1, bf16[768,512]{1,0:T(8,128)(2,1)S(1)} %get-tuple-element.48.kvs, ...), custom_call_target="tpu_custom_call" | custom-call | flops 3000000000 | bytes 4000000 | tf_op jit(solution)/shard_map/token_attention/pallas_call | solution.py:440
  85.9 8.2 %collective-permute-done.18.far_kvs = bf16[512,512]{1,0:T(8,128)(2,1)S(1)} collective-permute-done((bf16[512,512]{1,0:T(8,128)(2,1)S(1)}, bf16[512,512]{1,0:T(8,128)(2,1)S(1)}, u32[]{:S(2)}, u32[]{:S(2)}) %collective-permute-start.18) | collective-permute-done | bytes 524320 | tf_op jit(solution)/shard_map/ppermute | solution.py:566
  94.1 2.9 %token_attention.2 = (bf16[272,512]{1,0:T(8,128)(2,1)S(1)}, bf16[272,512]{1,0:T(8,128)(2,1)S(1)}) custom-call(s32[2,4096]{1,0:T(2,128)S(1)} %copy-done.3, bf16[256,512]{1,0:T(8,128)(2,1)S(1)} %get-tuple-element.32.q0.q, bf16[256,512]{1,0:T(8,128)(2,1)S(1)} %collective-permute-done.17.q1, bf16[768,512]{1,0:T(8,128)(2,1)S(1)} %get-tuple-element.40.kvs, ...), custom_call_target="tpu_custom_call" | custom-call | flops 3000000000 | bytes 4000000 | tf_op jit(solution)/shard_map/token_attention/pallas_call | solution.py:440
  102.0 3.4 %collective-permute-start.30 = (bf16[256,512]{1,0:T(8,128)(2,1)S(1)}, bf16[256,512]{1,0:T(8,128)(2,1)S(1)}, u32[]{:S(2)}, u32[]{:S(2)}) collective-permute-start(bf16[256,512]{1,0:T(8,128)(2,1)S(1)} %token_combine.3.a.refs_0_), channel_id=1, source_target_pairs={{0,1},{1,0},{2,3},{3,2},{4,5},{5,4},{6,7},{7,6},{8,9},{9,8},{10,11... | collective-permute-start | bytes 786440 | tf_op jit(solution)/shard_map/ppermute | solution.py:607
  105.9 4.0 %collective-permute-done.36.b = bf16[64,384]{1,0:T(8,128)(2,1)S(1)} collective-permute-done((bf16[64,384]{1,0:T(8,128)(2,1)S(1)}, bf16[64,384]{1,0:T(8,128)(2,1)S(1)}, u32[]{:S(2)}, u32[]{:S(2)}) %collective-permute-start.36) | collective-permute-done | bytes 49184 | tf_op jit(solution)/shard_map/ppermute | solution.py:587
  110.0 3.1 %collective-permute-start.37 = (bf16[32,512]{1,0:T(8,128)(2,1)S(1)}, bf16[32,512]{1,0:T(8,128)(2,1)S(1)}, u32[]{:S(2)}, u32[]{:S(2)}) collective-permute-start(bf16[32,512]{1,0:T(8,128)(2,1)S(1)} %memory_combine.11.a.o), channel_id=1, source_target_pairs={{0,1},{1,0},{2,3},{3,2},{4,5},{5,4},{6,7},{7,6},{8,9},{9,8},{10,11... | collective-permute-start | bytes 98312 | tf_op jit(solution)/shard_map/ppermute | solution.py:607
  117.0 3.4 %collective-permute-start.39 = (bf16[2,32,512]{2,1,0:T(8,128)(2,1)S(1)}, bf16[2,32,512]{2,1,0:T(8,128)(2,1)S(1)}, u32[]{:S(2)}, u32[]{:S(2)}) collective-permute-start(bf16[2,32,512]{2,1,0:T(8,128)(2,1)S(1)} %collective-permute-done.38.n), channel_id=1, source_target_pairs={{0,1},{1,0},{2,3},{3,2},{4,5},{5,4},{6,7},{7,6},{8,9},{9,8},{10,11... | collective-permute-start | bytes 196616 | tf_op jit(solution)/shard_map/ppermute | solution.py:607
  127.2 3.3 %collective-permute-done.31.v.refs_2_ = bf16[2,256,512]{2,1,0:T(8,128)(2,1)S(1)} collective-permute-done((bf16[2,256,512]{2,1,0:T(8,128)(2,1)S(1)}, bf16[2,256,512]{2,1,0:T(8,128)(2,1)S(1)}, u32[]{:S(2)}, u32[]{:S(2)}) %collective-permute-start.31) | collective-permute-done | bytes 524320 | tf_op jit(solution)/shard_map/ppermute | solution.py:603
  130.5 2.7 %collective-permute-start.33 = (bf16[256,512]{1,0:T(8,128)(2,1)S(1)}, bf16[256,512]{1,0:T(8,128)(2,1)S(1)}, u32[]{:S(2)}, u32[]{:S(2)}) collective-permute-start(bf16[256,512]{1,0:T(8,128)(2,1)S(1)} %first_of.3), channel_id=1, source_target_pairs={{0,2},{1,7},{2,4},{3,1},{4,6},{5,3},{6,0},{7,5},{8,10},{9,15},{10,... | collective-permute-start | bytes 786440 | tf_op jit(solution)/shard_map/ppermute | solution.py:603
  133.4 3.1 %collective-permute-start.45 = (bf16[32,1792]{1,0:T(8,128)(2,1)S(1)}, bf16[32,1792]{1,0:T(8,128)(2,1)S(1)}, u32[]{:S(2)}, u32[]{:S(2)}) collective-permute-start(bf16[32,1792]{1,0:T(8,128)(2,1)S(1)} %add_convert_fusion.1), channel_id=1, source_target_pairs={{0,4},{1,5},{2,6},{3,7},{4,0},{5,1},{6,2},{7,3},{8,12},{9,13},{10,... | collective-permute-start | bytes 344072 | tf_op jit(solution)/shard_map/ppermute | solution.py:599
  138.8 3.8 %collective-permute-done.43 = bf16[32,1792]{1,0:T(8,128)(2,1)S(1)} collective-permute-done((bf16[32,1792]{1,0:T(8,128)(2,1)S(1)}, bf16[32,1792]{1,0:T(8,128)(2,1)S(1)}, u32[]{:S(2)}, u32[]{:S(2)}) %collective-permute-start.43) | collective-permute-done | bytes 114720 | tf_op jit(solution)/shard_map/ppermute | solution.py:599
  (109 shorter events, 54.6 us)
Async XLA Ops:
  26.7 8.5 %collective-permute-start.5 = (bf16[2,32,512]{2,1,0:T(8,128)(2,1)S(1)}, bf16[2,32,512]{2,1,0:T(8,128)(2,1)S(1)}, u32[]{:S(2)}, u32[]{:S(2)}) collective-permute-start(bf16[2,32,512]{2,1,0:T(8,128)(2,1)S(1)} %pair_up.4), channel_id=1, source_target_pairs={{0,2},{1,7},{2,4},{3,1},{4,6},{5,3},{6,0},{7,5},{8,10},{9,15},{10,... | collective-permute-start | bytes 196616 | tf_op jit(solution)/shard_map/ppermute | solution.py:603
  34.8 8.8 %collective-permute-start.8 = (bf16[32,512]{1,0:T(8,128)(2,1)S(1)}, bf16[32,512]{1,0:T(8,128)(2,1)S(1)}, u32[]{:S(2)}, u32[]{:S(2)}) collective-permute-start(bf16[32,512]{1,0:T(8,128)(2,1)S(1)} %collective-permute-done.7.f), channel_id=1, source_target_pairs={{0,1},{1,0},{2,3},{3,2},{4,5},{5,4},{6,7},{7,6},{8,9},{9,8},{10,11... | collective-permute-start | bytes 98312 | tf_op jit(solution)/shard_map/ppermute | solution.py:607
  35.2 8.4 %collective-permute-start.6 = (bf16[2,32,512]{2,1,0:T(8,128)(2,1)S(1)}, bf16[2,32,512]{2,1,0:T(8,128)(2,1)S(1)}, u32[]{:S(2)}, u32[]{:S(2)}) collective-permute-start(bf16[2,32,512]{2,1,0:T(8,128)(2,1)S(1)} %collective-permute-done.5.n), channel_id=1, source_target_pairs={{0,1},{1,0},{2,3},{3,2},{4,5},{5,4},{6,7},{7,6},{8,9},{9,8},{10,11... | collective-permute-start | bytes 196616 | tf_op jit(solution)/shard_map/ppermute | solution.py:607
  39.4 8.6 %collective-permute-start.14 = (bf16[256,512]{1,0:T(8,128)(2,1)S(1)}, bf16[256,512]{1,0:T(8,128)(2,1)S(1)}, u32[]{:S(2)}, u32[]{:S(2)}) collective-permute-start(bf16[256,512]{1,0:T(8,128)(2,1)S(1)} %get-tuple-element.38.refs_0_.kvc), channel_id=1, source_target_pairs={{0,32},{8,40},{16,48},{24,56},{32,0},{40,8},{48,16},{56,24},{64,96... | collective-permute-start | bytes 786440 | tf_op jit(solution)/shard_map/ppermute | solution.py:566
  41.7 10.9 %collective-permute-start.26 = (bf16[256,512]{1,0:T(8,128)(2,1)S(1)}, bf16[256,512]{1,0:T(8,128)(2,1)S(1)}, u32[]{:S(2)}, u32[]{:S(2)}) collective-permute-start(bf16[256,512]{1,0:T(8,128)(2,1)S(1)} %get-tuple-element.47.kvc), channel_id=1, source_target_pairs={{0,32},{8,40},{16,48},{24,56},{32,64},{40,72},{48,80},{56,88},{64,... | collective-permute-start | bytes 786440 | tf_op jit(solution)/shard_map/ppermute | solution.py:574
  45.6 11.1 %collective-permute-start.9 = (bf16[32,1792]{1,0:T(8,128)(2,1)S(1)}, bf16[32,1792]{1,0:T(8,128)(2,1)S(1)}, u32[]{:S(2)}, u32[]{:S(2)}) collective-permute-start(bf16[32,1792]{1,0:T(8,128)(2,1)S(1)} %get-tuple-element.37), channel_id=1, source_target_pairs={{0,1},{1,0},{2,3},{3,2},{4,5},{5,4},{6,7},{7,6},{8,9},{9,8},{10,11... | collective-permute-start | bytes 344072 | tf_op jit(solution)/shard_map/ppermute | solution.py:607
  46.3 23.7 %collective-permute-start.16 = (bf16[256,512]{1,0:T(8,128)(2,1)S(1)}, bf16[256,512]{1,0:T(8,128)(2,1)S(1)}, u32[]{:S(2)}, u32[]{:S(2)}) collective-permute-start(bf16[256,512]{1,0:T(8,128)(2,1)S(1)} %get-tuple-element.38.refs_0_.kvc), channel_id=1, source_target_pairs={{0,96},{8,104},{16,112},{24,120},{32,64},{40,72},{48,80},{56,88},{... | collective-permute-start | bytes 786440 | tf_op jit(solution)/shard_map/ppermute | solution.py:566
  48.0 22.2 %collective-permute-start.15 = (bf16[256,512]{1,0:T(8,128)(2,1)S(1)}, bf16[256,512]{1,0:T(8,128)(2,1)S(1)}, u32[]{:S(2)}, u32[]{:S(2)}) collective-permute-start(bf16[256,512]{1,0:T(8,128)(2,1)S(1)} %collective-permute-done.14.refs_1_.kvb), channel_id=1, source_target_pairs={{0,96},{8,104},{16,112},{24,120},{32,64},{40,72},{48,80},{56,88},{... | collective-permute-start | bytes 786440 | tf_op jit(solution)/shard_map/ppermute | solution.py:566
  52.6 15.0 %collective-permute-start.27 = (bf16[256,512]{1,0:T(8,128)(2,1)S(1)}, bf16[256,512]{1,0:T(8,128)(2,1)S(1)}, u32[]{:S(2)}, u32[]{:S(2)}) collective-permute-start(bf16[256,512]{1,0:T(8,128)(2,1)S(1)} %collective-permute-done.26.kvb.kvb2), channel_id=1, source_target_pairs={{0,32},{8,40},{16,48},{24,56},{32,64},{40,72},{48,80},{56,88},{64,... | collective-permute-start | bytes 786440 | tf_op jit(solution)/shard_map/ppermute | solution.py:574
  56.7 13.6 %collective-permute-start.10 = (bf16[32,1792]{1,0:T(8,128)(2,1)S(1)}, bf16[32,1792]{1,0:T(8,128)(2,1)S(1)}, u32[]{:S(2)}, u32[]{:S(2)}) collective-permute-start(bf16[32,1792]{1,0:T(8,128)(2,1)S(1)} %add_convert_fusion.3), channel_id=1, source_target_pairs={{0,2},{1,3},{2,0},{3,1},{4,6},{5,7},{6,4},{7,5},{8,10},{9,11},{10,... | collective-permute-start | bytes 344072 | tf_op jit(solution)/shard_map/ppermute | solution.py:599
  57.4 14.5 %collective-permute-start.11 = (bf16[32,1792]{1,0:T(8,128)(2,1)S(1)}, bf16[32,1792]{1,0:T(8,128)(2,1)S(1)}, u32[]{:S(2)}, u32[]{:S(2)}) collective-permute-start(bf16[32,1792]{1,0:T(8,128)(2,1)S(1)} %add_convert_fusion.3), channel_id=1, source_target_pairs={{0,6},{1,7},{2,4},{3,5},{4,2},{5,3},{6,0},{7,1},{8,14},{9,15},{10,... | collective-permute-start | bytes 344072 | tf_op jit(solution)/shard_map/ppermute | solution.py:599
  70.0 12.9 %collective-permute-start.28 = (bf16[512,512]{1,0:T(8,128)(2,1)S(1)}, bf16[512,512]{1,0:T(8,128)(2,1)S(1)}, u32[]{:S(2)}, u32[]{:S(2)}) collective-permute-start(bf16[512,512]{1,0:T(8,128)(2,1)S(1)} %get-tuple-element.49), channel_id=1, source_target_pairs={{0,24},{8,16},{16,8},{24,0},{32,56},{40,48},{48,40},{56,32},{64,88... | collective-permute-start | bytes 1572872 | tf_op jit(solution)/shard_map/ppermute | solution.py:566
  70.4 15.5 %collective-permute-start.17 = (bf16[256,512]{1,0:T(8,128)(2,1)S(1)}, bf16[256,512]{1,0:T(8,128)(2,1)S(1)}, u32[]{:S(2)}, u32[]{:S(2)}) collective-permute-start(bf16[256,512]{1,0:T(8,128)(2,1)S(1)} %get-tuple-element.32.q0.q), channel_id=1, source_target_pairs={{0,8},{8,0},{16,24},{24,16},{32,40},{40,32},{48,56},{56,48},{64,72... | collective-permute-start | bytes 786440 | tf_op jit(solution)/shard_map/ppermute | solution.py:566
  71.9 22.1 %collective-permute-start.18 = (bf16[512,512]{1,0:T(8,128)(2,1)S(1)}, bf16[512,512]{1,0:T(8,128)(2,1)S(1)}, u32[]{:S(2)}, u32[]{:S(2)}) collective-permute-start(bf16[512,512]{1,0:T(8,128)(2,1)S(1)} %get-tuple-element.41), channel_id=1, source_target_pairs={{0,24},{8,16},{16,8},{24,0},{32,56},{40,48},{48,40},{56,32},{64,88... | collective-permute-start | bytes 1572872 | tf_op jit(solution)/shard_map/ppermute | solution.py:566
  74.5 22.6 %collective-permute-start.13 = (bf16[32,1792]{1,0:T(8,128)(2,1)S(1)}, bf16[32,1792]{1,0:T(8,128)(2,1)S(1)}, u32[]{:S(2)}, u32[]{:S(2)}) collective-permute-start(bf16[32,1792]{1,0:T(8,128)(2,1)S(1)} %add_convert_fusion.2.own), channel_id=1, source_target_pairs={{0,1},{1,0},{2,3},{3,2},{4,5},{5,4},{6,7},{7,6},{8,9},{9,8},{10,11... | collective-permute-start | bytes 344072 | tf_op jit(solution)/shard_map/ppermute | solution.py:607
  85.8 15.2 %collective-permute-start.29 = (bf16[272,512]{1,0:T(8,128)(2,1)S(1)}, bf16[272,512]{1,0:T(8,128)(2,1)S(1)}, u32[]{:S(2)}, u32[]{:S(2)}) collective-permute-start(bf16[272,512]{1,0:T(8,128)(2,1)S(1)} %get-tuple-element.51), channel_id=1, source_target_pairs={{0,8},{8,0},{16,24},{24,16},{32,40},{40,32},{48,56},{56,48},{64,72... | collective-permute-start | bytes 835592 | tf_op jit(solution)/shard_map/ppermute | solution.py:566
  97.0 23.4 %collective-permute-start.19 = (bf16[272,512]{1,0:T(8,128)(2,1)S(1)}, bf16[272,512]{1,0:T(8,128)(2,1)S(1)}, u32[]{:S(2)}, u32[]{:S(2)}) collective-permute-start(bf16[272,512]{1,0:T(8,128)(2,1)S(1)} %get-tuple-element.43), channel_id=1, source_target_pairs={{0,8},{8,0},{16,24},{24,16},{32,40},{40,32},{48,56},{56,48},{64,72... | collective-permute-start | bytes 835592 | tf_op jit(solution)/shard_map/ppermute | solution.py:566
  102.0 20.1 %collective-permute-start.30 = (bf16[256,512]{1,0:T(8,128)(2,1)S(1)}, bf16[256,512]{1,0:T(8,128)(2,1)S(1)}, u32[]{:S(2)}, u32[]{:S(2)}) collective-permute-start(bf16[256,512]{1,0:T(8,128)(2,1)S(1)} %token_combine.3.a.refs_0_), channel_id=1, source_target_pairs={{0,1},{1,0},{2,3},{3,2},{4,5},{5,4},{6,7},{7,6},{8,9},{9,8},{10,11... | collective-permute-start | bytes 786440 | tf_op jit(solution)/shard_map/ppermute | solution.py:607
  125.9 10.7 %collective-permute-start.21 = (bf16[2,256,512]{2,1,0:T(8,128)(2,1)S(1)}, bf16[2,256,512]{2,1,0:T(8,128)(2,1)S(1)}, u32[]{:S(2)}, u32[]{:S(2)}) collective-permute-start(bf16[2,256,512]{2,1,0:T(8,128)(2,1)S(1)} %pair_up.5), channel_id=1, source_target_pairs={{0,2},{1,7},{2,4},{3,1},{4,6},{5,3},{6,0},{7,5},{8,10},{9,15},{10,... | collective-permute-start | bytes 1572872 | tf_op jit(solution)/shard_map/ppermute | solution.py:603
  130.5 14.2 %collective-permute-start.33 = (bf16[256,512]{1,0:T(8,128)(2,1)S(1)}, bf16[256,512]{1,0:T(8,128)(2,1)S(1)}, u32[]{:S(2)}, u32[]{:S(2)}) collective-permute-start(bf16[256,512]{1,0:T(8,128)(2,1)S(1)} %first_of.3), channel_id=1, source_target_pairs={{0,2},{1,7},{2,4},{3,1},{4,6},{5,3},{6,0},{7,5},{8,10},{9,15},{10,... | collective-permute-start | bytes 786440 | tf_op jit(solution)/shard_map/ppermute | solution.py:603
  133.2 9.4 %collective-permute-start.43 = (bf16[32,1792]{1,0:T(8,128)(2,1)S(1)}, bf16[32,1792]{1,0:T(8,128)(2,1)S(1)}, u32[]{:S(2)}, u32[]{:S(2)}) collective-permute-start(bf16[32,1792]{1,0:T(8,128)(2,1)S(1)} %add_convert_fusion.1), channel_id=1, source_target_pairs={{0,2},{1,3},{2,0},{3,1},{4,6},{5,7},{6,4},{7,5},{8,10},{9,11},{10,... | collective-permute-start | bytes 344072 | tf_op jit(solution)/shard_map/ppermute | solution.py:599
  133.3 10.0 %collective-permute-start.44 = (bf16[32,1792]{1,0:T(8,128)(2,1)S(1)}, bf16[32,1792]{1,0:T(8,128)(2,1)S(1)}, u32[]{:S(2)}, u32[]{:S(2)}) collective-permute-start(bf16[32,1792]{1,0:T(8,128)(2,1)S(1)} %add_convert_fusion.1), channel_id=1, source_target_pairs={{0,6},{1,7},{2,4},{3,5},{4,2},{5,3},{6,0},{7,1},{8,14},{9,15},{10,... | collective-permute-start | bytes 344072 | tf_op jit(solution)/shard_map/ppermute | solution.py:599
  133.4 11.3 %collective-permute-start.45 = (bf16[32,1792]{1,0:T(8,128)(2,1)S(1)}, bf16[32,1792]{1,0:T(8,128)(2,1)S(1)}, u32[]{:S(2)}, u32[]{:S(2)}) collective-permute-start(bf16[32,1792]{1,0:T(8,128)(2,1)S(1)} %add_convert_fusion.1), channel_id=1, source_target_pairs={{0,4},{1,5},{2,6},{3,7},{4,0},{5,1},{6,2},{7,3},{8,12},{9,13},{10,... | collective-permute-start | bytes 344072 | tf_op jit(solution)/shard_map/ppermute | solution.py:599
  136.6 10.2 %collective-permute-start.22 = (bf16[256,512]{1,0:T(8,128)(2,1)S(1)}, bf16[256,512]{1,0:T(8,128)(2,1)S(1)}, u32[]{:S(2)}, u32[]{:S(2)}) collective-permute-start(bf16[256,512]{1,0:T(8,128)(2,1)S(1)} %first_of.2), channel_id=1, source_target_pairs={{0,2},{1,7},{2,4},{3,1},{4,6},{5,3},{6,0},{7,5},{8,10},{9,15},{10,... | collective-permute-start | bytes 786440 | tf_op jit(solution)/shard_map/ppermute | solution.py:603
  (27 other events, 171.7 us)
where the time goes:
time: 154 us; the launch traced here: 153 us
  starting transfers between devices  64.9 us (42%)
  waiting for transfers between devices  57.4 us (37%)
  Pallas kernels  29.2 us (19%)
    ppermute x16, starting transfers between devices, other_core(): return lax.ppermute(v, 'head', [(i, i ^ 1) for i in range(N_HEAD)])  25.4 us
    ppermute x9, waiting for transfers between devices, x_xor(): return lax.ppermute(v, 'seq', [(i, i ^ d) for i in range(N_SEQ)])  13.3 us
    ppermute x2, waiting for transfers between devices, y_later(): lax.ppermute(v, 'seq', [(i, i + SHAPE) for i in range(N_SEQ - SHAPE)])  12.8 us
    ppermute x6, starting transfers between devices, z_turn(): lax.ppermute(v, 'head', [(i, (i + 2 - 4 * (i % 2)) % N_HEAD) for i in ran...  12.5 us
    ppermute x8, waiting for transfers between devices, z_xor(): return lax.ppermute(v, 'head', [(i, i ^ 2 * d) for i in range(N_HEAD)])  8.88 us
    ppermute x9, starting transfers between devices, x_xor(): return lax.ppermute(v, 'seq', [(i, i ^ d) for i in range(N_SEQ)])  8.5 us
    ppermute x8, starting transfers between devices, z_xor(): return lax.ppermute(v, 'head', [(i, i ^ 2 * d) for i in range(N_HEAD)])  8.49 us
    ppermute x2, waiting for transfers between devices, x_far(): return lax.ppermute(v, 'seq', [(i, i ^ 3) for i in range(N_SEQ)])  7.91 us
  transfers between devices with their start and end apart: 47, of which 16 were waited for; matrix products, arithmetic and copies ran while one was open for 0% of the time, Pallas kernels for 15%

commit v1 on v0

--- a/solution.py
+++ b/solution.py
@@ -396,7 +396,7 @@
     )(kva, kvb, kvb2, kvc)
 
 
-def token_kernel(seg, docs, q0, q1, kvs, far_kvs, o0, o1, kcode):
+def token_kernel(seg, e, docs, q_ref, kvs, far_kvs, o_ref, kcode):
     x, y, _, _ = place()
     lane = lax.broadcasted_iota(jnp.int32, (1, ROWS), 1).astype(F32)
 
@@ -412,43 +412,42 @@
         code = codes_of(block)[1]
         kcode[:, n * ROWS : (n + 1) * ROWS] = jnp.where(block >= 0, code, -1.0)
     near = lax.bitwise_xor(x, 1)
-    for e, (q_ref, o_ref) in enumerate(((q0, o0), (q1, o1))):
-        low, high = codes_of(y * SHAPE + (x if e == 0 else near))
-        low, high = column(low), column(high)
-        if e == 0:
-            span = slice(0, 3 * ROWS)
-        else:
-            span = pl.ds(pl.multiple_of(jnp.where(near < x, 0, ROWS), ROWS), 2 * ROWS)
-        keys = [kvs[span, :], far_kvs[...]]
-        codes = [kcode[:, span], kcode[:, 3 * ROWS :]]
-        valid = [(k >= low) & (k <= high) for k in codes]
-        for g in range(2):
-            q = q_ref[:, g * HD : (g + 1) * HD]
-            scores = [
-                jnp.where(v, dot_t(q, k[:, :HD]) * LOG2E_SCALE, LOW) for v, k in zip(valid, keys)
-            ]
-            out, lse = attend(scores, [k[:, HD:] for k in keys])
-            row = as_row(lse)
-            hi = row.astype(BF).astype(F32)
-            sub = lax.broadcasted_iota(jnp.int32, (16, ROWS), 0)
-            stats = jnp.where(sub == 0, hi, jnp.where(sub == 1, row - hi, 0.0))
-            o_ref[:ROWS, g * HD : (g + 1) * HD] = out.astype(BF)
-            o_ref[ROWS:, g * HD : (g + 1) * HD] = stats.astype(BF)
-
-
-def token_attention(docs, seg, q, near_q, kvs, far_kvs):
-    return pl.pallas_call(
-        functools.partial(token_kernel, seg),
-        in_specs=[WHOLE] * 5,
-        out_specs=[WHOLE] * 2,
-        out_shape=[jax.ShapeDtypeStruct((ROWS + 16, 2 * HD), BF)] * 2,
+    low, high = codes_of(y * SHAPE + (x if e == 0 else near))
+    low, high = column(low), column(high)
+    if e == 0:
+        span = slice(0, 3 * ROWS)
+    else:
+        span = pl.ds(pl.multiple_of(jnp.where(near < x, 0, ROWS), ROWS), 2 * ROWS)
+    keys = [kvs[span, :], far_kvs[...]]
+    codes = [kcode[:, span], kcode[:, 3 * ROWS :]]
+    valid = [(k >= low) & (k <= high) for k in codes]
+    for g in range(2):
+        q = q_ref[:, g * HD : (g + 1) * HD]
+        scores = [
+            jnp.where(v, dot_t(q, k[:, :HD]) * LOG2E_SCALE, LOW) for v, k in zip(valid, keys)
+        ]
+        out, lse = attend(scores, [k[:, HD:] for k in keys])
+        row = as_row(lse)
+        hi = row.astype(BF).astype(F32)
+        sub = lax.broadcasted_iota(jnp.int32, (16, ROWS), 0)
+        stats = jnp.where(sub == 0, hi, jnp.where(sub == 1, row - hi, 0.0))
+        o_ref[:ROWS, g * HD : (g + 1) * HD] = out.astype(BF)
+        o_ref[ROWS:, g * HD : (g + 1) * HD] = stats.astype(BF)
+
+
+def token_attention(docs, seg, e, q, kvs, far_kvs):
+    return pl.pallas_call(
+        functools.partial(token_kernel, seg, e),
+        in_specs=[WHOLE] * 4,
+        out_specs=WHOLE,
+        out_shape=jax.ShapeDtypeStruct((ROWS + 16, 2 * HD), BF),
         scratch_shapes=[pltpu.VMEM((1, 5 * ROWS), F32)],
         compiler_params=params(16),
         cost_estimate=pl.CostEstimate(
             flops=3 * 10**9, bytes_accessed=4 * 10**6, transcendentals=10**6
         ),
         name="token_attention",
-    )(docs, q, near_q, kvs, far_kvs)
+    )(docs, q, kvs, far_kvs)
 
 
 def token_combine_kernel(q, qkvm, a, b, out_ref):
@@ -665,7 +664,9 @@
         near_q = x_xor(own_q, 1)
         stacked, send = stack(kvs[2], kvs[1], kvs[-1], kvs[0])
         far_kvs = x_xor(send, 3)
-        mine, send = token_attention(doc_ids, s, own_q, near_q, stacked, far_kvs)
+        keys = (stacked, far_kvs)
+        send = token_attention(doc_ids, s, 1, near_q, *keys)
+        mine = token_attention(doc_ids, s, 0, own_q, *keys)
         parts = [mine, x_xor(send, 1)]
         attn = token_combine(own_q, qkvm, parts)
         blocks = gather_heads(attn)

time: 154 us -> 145 us (0.942)
  the two profiles are of different devices: /device:TPU:23 before, /device:TPU:1 now
where the time goes in v1:
time: 145 us
  starting transfers between devices  69.3 us (48%)
  waiting for transfers between devices  43.7 us (30%)
  Pallas kernels  30.2 us (21%)
    ppermute x16, starting transfers between devices, other_core(): return lax.ppermute(v, 'head', [(i, i ^ 1) for i in range(N_HEAD)])  20.5 us
    ppermute x9, starting transfers between devices, x_xor(): return lax.ppermute(v, 'seq', [(i, i ^ d) for i in range(N_SEQ)])  13.4 us
    ppermute x6, starting transfers between devices, z_turn(): lax.ppermute(v, 'head', [(i, (i + 2 - 4 * (i % 2)) % N_HEAD) for i in ran...  13.1 us
    ppermute x2, waiting for transfers between devices, x_far(): return lax.ppermute(v, 'seq', [(i, i ^ 3) for i in range(N_SEQ)])  12.7 us
    ppermute x8, waiting for transfers between devices, z_xor(): return lax.ppermute(v, 'head', [(i, i ^ 2 * d) for i in range(N_HEAD)])  9.71 us
    ppermute x8, starting transfers between devices, z_xor(): return lax.ppermute(v, 'head', [(i, i ^ 2 * d) for i in range(N_HEAD)])  8.17 us
    pallas_call x4, Pallas kernels, token_attention(): pl.pallas_call(functools.partial(token_kernel, seg, e), in_specs=[WHOLE]...  6.82 us
    ppermute x9, waiting for transfers between devices, x_xor(): return lax.ppermute(v, 'seq', [(i, i ^ d) for i in range(N_SEQ)])  6.73 us
  transfers between devices with their start and end apart: 47, of which 20 were waited for; matrix products, arithmetic and copies ran while one was open for 0% of the time, Pallas kernels for 16%

profile of v1, /device:TPU:1, one launch (start us, length us, event | category | flops | bytes accessed | tf_op | source)
XLA Modules:
  0.0 145.0 jit_solution(2241208471932062487)
XLA Ops:
  1.3 5.1 %first_project.1 = (bf16[256,512]{1,0:T(8,128)(2,1)S(1)}, bf16[256,512]{1,0:T(8,128)(2,1)S(1)}, bf16[32,1024]{1,0:T(8,128)(2,1)S(1)}, bf16[64,384]{1,0:T(8,128)(...) custom-call(bf16[2,256,3584]{2,1,0:T(8,128)(2,1)} %x.3, ...), custom_call_target="tpu_custom_call" | custom-call | flops 2113929216 | bytes 10485760 | tf_op jit(solution)/shard_map/first_project/pallas_call | solution.py:147
  10.2 2.8 %collective-permute-start.1 = (bf16[64,384]{1,0:T(8,128)(2,1)S(1)}, bf16[64,384]{1,0:T(8,128)(2,1)S(1)}, u32[]{:S(2)}, u32[]{:S(2)}) collective-permute-start(bf16[64,384]{1,0:T(8,128)(2,1)S(1)} %memory_combine.6.a), channel_id=1, source_target_pairs={{0,24},{8,16},{16,8},{24,0},{32,56},{40,48},{48,40},{56,32},{64,88... | collective-permute-start | bytes 147464 | tf_op jit(solution)/shard_map/ppermute | solution.py:586
  17.9 3.0 %collective-permute-start.3 = (bf16[64,384]{1,0:T(8,128)(2,1)S(1)}, bf16[64,384]{1,0:T(8,128)(2,1)S(1)}, u32[]{:S(2)}, u32[]{:S(2)}) collective-permute-start(bf16[64,384]{1,0:T(8,128)(2,1)S(1)} %memory_combine.8.a), channel_id=1, source_target_pairs={{0,96},{8,104},{16,112},{24,120},{32,64},{40,72},{48,80},{56,88},{... | collective-permute-start | bytes 147464 | tf_op jit(solution)/shard_map/ppermute | solution.py:594
  22.6 5.2 %collective-permute-start.4 = (bf16[32,512]{1,0:T(8,128)(2,1)S(1)}, bf16[32,512]{1,0:T(8,128)(2,1)S(1)}, u32[]{:S(2)}, u32[]{:S(2)}) collective-permute-start(bf16[32,512]{1,0:T(8,128)(2,1)S(1)} %memory_combine.9.a.o), channel_id=1, source_target_pairs={{0,1},{1,0},{2,3},{3,2},{4,5},{5,4},{6,7},{7,6},{8,9},{9,8},{10,11... | collective-permute-start | bytes 98312 | tf_op jit(solution)/shard_map/ppermute | solution.py:606
  28.6 3.9 %collective-permute-start.5 = (bf16[2,32,512]{2,1,0:T(8,128)(2,1)S(1)}, bf16[2,32,512]{2,1,0:T(8,128)(2,1)S(1)}, u32[]{:S(2)}, u32[]{:S(2)}) collective-permute-start(bf16[2,32,512]{2,1,0:T(8,128)(2,1)S(1)} %pair_up.4), channel_id=1, source_target_pairs={{0,2},{1,7},{2,4},{3,1},{4,6},{5,3},{6,0},{7,5},{8,10},{9,15},{10,... | collective-permute-start | bytes 196616 | tf_op jit(solution)/shard_map/ppermute | solution.py:602
  34.5 2.4 %collective-permute-done.7.f = bf16[32,512]{1,0:T(8,128)(2,1)S(1)} collective-permute-done((bf16[32,512]{1,0:T(8,128)(2,1)S(1)}, bf16[32,512]{1,0:T(8,128)(2,1)S(1)}, u32[]{:S(2)}, u32[]{:S(2)}) %collective-permute-start.7) | collective-permute-done | bytes 32800 | tf_op jit(solution)/shard_map/ppermute | solution.py:598
  37.4 4.0 %second_project.1 = (bf16[256,512]{1,0:T(8,128)(2,1)S(1)}, bf16[256,512]{1,0:T(8,128)(2,1)S(1)}, bf16[448,4096]{1,0:T(8,128)(2,1)S(1)}, bf16[448,3584]{1,0:T(8,128)(2,1)S(1)}, bf16[2,256,512]{2,1,0:T(8,128)(2,1)S(1)}) custom-call(bf16[2,256,3584]{2,1,0:T(8,128)(2,1)} %x.3, bf16[3584]{0:T(1024)(128)(2,1)S(1)} %copy-done.1, ...), custom_call_target="tpu_custom_call" | custom-call | flops 1879048192 | bytes 10485760 | tf_op jit(solution)/shard_map/second_project/pallas_call | solution.py:206
  44.8 2.4 %collective-permute-start.26 = (bf16[256,512]{1,0:T(8,128)(2,1)S(1)}, bf16[256,512]{1,0:T(8,128)(2,1)S(1)}, u32[]{:S(2)}, u32[]{:S(2)}) collective-permute-start(bf16[256,512]{1,0:T(8,128)(2,1)S(1)} %collective-permute-done.25.kvb.kvb2), channel_id=1, source_target_pairs={{0,32},{8,40},{16,48},{24,56},{32,64},{40,72},{48,80},{56,88},{64,... | collective-permute-start | bytes 786440 | tf_op jit(solution)/shard_map/ppermute | solution.py:573
  51.6 2.7 %collective-permute-start.16 = (bf16[256,512]{1,0:T(8,128)(2,1)S(1)}, bf16[256,512]{1,0:T(8,128)(2,1)S(1)}, u32[]{:S(2)}, u32[]{:S(2)}) collective-permute-start(bf16[256,512]{1,0:T(8,128)(2,1)S(1)} %get-tuple-element.34.refs_0_.kvc), channel_id=1, source_target_pairs={{0,96},{8,104},{16,112},{24,120},{32,64},{40,72},{48,80},{56,88},{... | collective-permute-start | bytes 786440 | tf_op jit(solution)/shard_map/ppermute | solution.py:565
  56.0 3.9 %collective-permute-start.15 = (bf16[256,512]{1,0:T(8,128)(2,1)S(1)}, bf16[256,512]{1,0:T(8,128)(2,1)S(1)}, u32[]{:S(2)}, u32[]{:S(2)}) collective-permute-start(bf16[256,512]{1,0:T(8,128)(2,1)S(1)} %collective-permute-done.14.refs_1_.kvb), channel_id=1, source_target_pairs={{0,96},{8,104},{16,112},{24,120},{32,64},{40,72},{48,80},{56,88},{... | collective-permute-start | bytes 786440 | tf_op jit(solution)/shard_map/ppermute | solution.py:565
  60.0 2.6 %collective-permute-start.27 = (bf16[512,512]{1,0:T(8,128)(2,1)S(1)}, bf16[512,512]{1,0:T(8,128)(2,1)S(1)}, u32[]{:S(2)}, u32[]{:S(2)}) collective-permute-start(bf16[512,512]{1,0:T(8,128)(2,1)S(1)} %get-tuple-element.43), channel_id=1, source_target_pairs={{0,24},{8,16},{16,8},{24,0},{32,56},{40,48},{48,40},{56,32},{64,88... | collective-permute-start | bytes 1572872 | tf_op jit(solution)/shard_map/ppermute | solution.py:565
  65.7 2.7 %collective-permute-start.17 = (bf16[512,512]{1,0:T(8,128)(2,1)S(1)}, bf16[512,512]{1,0:T(8,128)(2,1)S(1)}, u32[]{:S(2)}, u32[]{:S(2)}) collective-permute-start(bf16[512,512]{1,0:T(8,128)(2,1)S(1)} %get-tuple-element.37), channel_id=1, source_target_pairs={{0,24},{8,16},{16,8},{24,0},{32,56},{40,48},{48,40},{56,32},{64,88... | collective-permute-start | bytes 1572872 | tf_op jit(solution)/shard_map/ppermute | solution.py:565
  68.5 2.4 %memory_project.1 = (bf16[32,1024]{1,0:T(8,128)(2,1)S(1)}, bf16[64,384]{1,0:T(8,128)(2,1)S(1)}, bf16[32,3584]{1,0:T(8,128)(2,1)S(1)}) custom-call(bf16[32,1792]{1,0:T(8,128)(2,1)S(1)} %add_convert_fusion.2.own, bf16[32,1792]{1,0:T(8,128)(2,1)S(1)} %collective-permute-done.13.other, bf16[3584]{0:T(1024)(128)(2,1)S(1)} %copy-done.2, ...), custom_call_target="tpu_custom_call" | custom-call | flops 1879048192 | bytes 8388608 | tf_op jit(solution)/shard_map/memory_project/pallas_call | solution.py:239
  70.9 3.2 %collective-permute-done.35.b = bf16[64,384]{1,0:T(8,128)(2,1)S(1)} collective-permute-done((bf16[64,384]{1,0:T(8,128)(2,1)S(1)}, bf16[64,384]{1,0:T(8,128)(2,1)S(1)}, u32[]{:S(2)}, u32[]{:S(2)}) %collective-permute-start.35) | collective-permute-done | bytes 49184 | tf_op jit(solution)/shard_map/ppermute | solution.py:582
  74.6 11.2 %collective-permute-done.36.b = bf16[64,384]{1,0:T(8,128)(2,1)S(1)} collective-permute-done((bf16[64,384]{1,0:T(8,128)(2,1)S(1)}, bf16[64,384]{1,0:T(8,128)(2,1)S(1)}, u32[]{:S(2)}, u32[]{:S(2)}) %collective-permute-start.36) | collective-permute-done | bytes 49184 | tf_op jit(solution)/shard_map/ppermute | solution.py:586
  86.0 2.2 %collective-permute-start.37 = (bf16[32,512]{1,0:T(8,128)(2,1)S(1)}, bf16[32,512]{1,0:T(8,128)(2,1)S(1)}, u32[]{:S(2)}, u32[]{:S(2)}) collective-permute-start(bf16[32,512]{1,0:T(8,128)(2,1)S(1)} %memory_combine.11.a.o), channel_id=1, source_target_pairs={{0,1},{1,0},{2,3},{3,2},{4,5},{5,4},{6,7},{7,6},{8,9},{9,8},{10,11... | collective-permute-start | bytes 98312 | tf_op jit(solution)/shard_map/ppermute | solution.py:606
  91.7 2.8 %collective-permute-done.40.f = bf16[32,512]{1,0:T(8,128)(2,1)S(1)} collective-permute-done((bf16[32,512]{1,0:T(8,128)(2,1)S(1)}, bf16[32,512]{1,0:T(8,128)(2,1)S(1)}, u32[]{:S(2)}, u32[]{:S(2)}) %collective-permute-start.40) | collective-permute-done | bytes 32800 | tf_op jit(solution)/shard_map/ppermute | solution.py:598
  102.8 2.5 %collective-permute-done.29.b = bf16[272,512]{1,0:T(8,128)(2,1)S(1)} collective-permute-done((bf16[272,512]{1,0:T(8,128)(2,1)S(1)}, bf16[272,512]{1,0:T(8,128)(2,1)S(1)}, u32[]{:S(2)}, u32[]{:S(2)}) %collective-permute-start.29) | collective-permute-done | bytes 278560 | tf_op jit(solution)/shard_map/ppermute | solution.py:565
  106.3 2.6 %collective-permute-start.30 = (bf16[256,512]{1,0:T(8,128)(2,1)S(1)}, bf16[256,512]{1,0:T(8,128)(2,1)S(1)}, u32[]{:S(2)}, u32[]{:S(2)}) collective-permute-start(bf16[256,512]{1,0:T(8,128)(2,1)S(1)} %token_combine.3.a.refs_0_), channel_id=1, source_target_pairs={{0,1},{1,0},{2,3},{3,2},{4,5},{5,4},{6,7},{7,6},{8,9},{9,8},{10,11... | collective-permute-start | bytes 786440 | tf_op jit(solution)/shard_map/ppermute | solution.py:606
  118.9 3.3 %collective-permute-done.31.v.refs_2_ = bf16[2,256,512]{2,1,0:T(8,128)(2,1)S(1)} collective-permute-done((bf16[2,256,512]{2,1,0:T(8,128)(2,1)S(1)}, bf16[2,256,512]{2,1,0:T(8,128)(2,1)S(1)}, u32[]{:S(2)}, u32[]{:S(2)}) %collective-permute-start.31) | collective-permute-done | bytes 524320 | tf_op jit(solution)/shard_map/ppermute | solution.py:602
  122.2 2.8 %collective-permute-start.33 = (bf16[256,512]{1,0:T(8,128)(2,1)S(1)}, bf16[256,512]{1,0:T(8,128)(2,1)S(1)}, u32[]{:S(2)}, u32[]{:S(2)}) collective-permute-start(bf16[256,512]{1,0:T(8,128)(2,1)S(1)} %first_of.3), channel_id=1, source_target_pairs={{0,2},{1,7},{2,4},{3,1},{4,6},{5,3},{6,0},{7,5},{8,10},{9,15},{10,... | collective-permute-start | bytes 786440 | tf_op jit(solution)/shard_map/ppermute | solution.py:602
  125.8 2.6 %collective-permute-start.45 = (bf16[32,1792]{1,0:T(8,128)(2,1)S(1)}, bf16[32,1792]{1,0:T(8,128)(2,1)S(1)}, u32[]{:S(2)}, u32[]{:S(2)}) collective-permute-start(bf16[32,1792]{1,0:T(8,128)(2,1)S(1)} %add_convert_fusion.1), channel_id=1, source_target_pairs={{0,4},{1,5},{2,6},{3,7},{4,0},{5,1},{6,2},{7,3},{8,12},{9,13},{10,... | collective-permute-start | bytes 344072 | tf_op jit(solution)/shard_map/ppermute | solution.py:598
  128.4 2.2 %collective-permute-start.22 = (bf16[256,512]{1,0:T(8,128)(2,1)S(1)}, bf16[256,512]{1,0:T(8,128)(2,1)S(1)}, u32[]{:S(2)}, u32[]{:S(2)}) collective-permute-start(bf16[256,512]{1,0:T(8,128)(2,1)S(1)} %first_of.2), channel_id=1, source_target_pairs={{0,2},{1,7},{2,4},{3,1},{4,6},{5,3},{6,0},{7,5},{8,10},{9,15},{10,... | collective-permute-start | bytes 786440 | tf_op jit(solution)/shard_map/ppermute | solution.py:602
  130.6 3.7 %collective-permute-done.43 = bf16[32,1792]{1,0:T(8,128)(2,1)S(1)} collective-permute-done((bf16[32,1792]{1,0:T(8,128)(2,1)S(1)}, bf16[32,1792]{1,0:T(8,128)(2,1)S(1)}, u32[]{:S(2)}, u32[]{:S(2)}) %collective-permute-start.43) | collective-permute-done | bytes 114720 | tf_op jit(solution)/shard_map/ppermute | solution.py:598
  (111 shorter events, 61.8 us)
Async XLA Ops:
  28.6 8.6 %collective-permute-start.5 = (bf16[2,32,512]{2,1,0:T(8,128)(2,1)S(1)}, bf16[2,32,512]{2,1,0:T(8,128)(2,1)S(1)}, u32[]{:S(2)}, u32[]{:S(2)}) collective-permute-start(bf16[2,32,512]{2,1,0:T(8,128)(2,1)S(1)} %pair_up.4), channel_id=1, source_target_pairs={{0,2},{1,7},{2,4},{3,1},{4,6},{5,3},{6,0},{7,5},{8,10},{9,15},{10,... | collective-permute-start | bytes 196616 | tf_op jit(solution)/shard_map/ppermute | solution.py:602
  32.5 12.3 %collective-permute-start.25 = (bf16[256,512]{1,0:T(8,128)(2,1)S(1)}, bf16[256,512]{1,0:T(8,128)(2,1)S(1)}, u32[]{:S(2)}, u32[]{:S(2)}) collective-permute-start(bf16[256,512]{1,0:T(8,128)(2,1)S(1)} %get-tuple-element.41.kvc), channel_id=1, source_target_pairs={{0,32},{8,40},{16,48},{24,56},{32,64},{40,72},{48,80},{56,88},{64,... | collective-permute-start | bytes 786440 | tf_op jit(solution)/shard_map/ppermute | solution.py:573
  44.8 11.2 %collective-permute-start.26 = (bf16[256,512]{1,0:T(8,128)(2,1)S(1)}, bf16[256,512]{1,0:T(8,128)(2,1)S(1)}, u32[]{:S(2)}, u32[]{:S(2)}) collective-permute-start(bf16[256,512]{1,0:T(8,128)(2,1)S(1)} %collective-permute-done.25.kvb.kvb2), channel_id=1, source_target_pairs={{0,32},{8,40},{16,48},{24,56},{32,64},{40,72},{48,80},{56,88},{64,... | collective-permute-start | bytes 786440 | tf_op jit(solution)/shard_map/ppermute | solution.py:573
  47.3 12.8 %collective-permute-start.10 = (bf16[32,1792]{1,0:T(8,128)(2,1)S(1)}, bf16[32,1792]{1,0:T(8,128)(2,1)S(1)}, u32[]{:S(2)}, u32[]{:S(2)}) collective-permute-start(bf16[32,1792]{1,0:T(8,128)(2,1)S(1)} %add_convert_fusion.3), channel_id=1, source_target_pairs={{0,2},{1,3},{2,0},{3,1},{4,6},{5,7},{6,4},{7,5},{8,10},{9,11},{10,... | collective-permute-start | bytes 344072 | tf_op jit(solution)/shard_map/ppermute | solution.py:598
  48.1 14.4 %collective-permute-start.11 = (bf16[32,1792]{1,0:T(8,128)(2,1)S(1)}, bf16[32,1792]{1,0:T(8,128)(2,1)S(1)}, u32[]{:S(2)}, u32[]{:S(2)}) collective-permute-start(bf16[32,1792]{1,0:T(8,128)(2,1)S(1)} %add_convert_fusion.3), channel_id=1, source_target_pairs={{0,6},{1,7},{2,4},{3,5},{4,2},{5,3},{6,0},{7,1},{8,14},{9,15},{10,... | collective-permute-start | bytes 344072 | tf_op jit(solution)/shard_map/ppermute | solution.py:598
  50.1 12.5 %collective-permute-start.12 = (bf16[32,1792]{1,0:T(8,128)(2,1)S(1)}, bf16[32,1792]{1,0:T(8,128)(2,1)S(1)}, u32[]{:S(2)}, u32[]{:S(2)}) collective-permute-start(bf16[32,1792]{1,0:T(8,128)(2,1)S(1)} %add_convert_fusion.3), channel_id=1, source_target_pairs={{0,4},{1,5},{2,6},{3,7},{4,0},{5,1},{6,2},{7,3},{8,12},{9,13},{10,... | collective-permute-start | bytes 344072 | tf_op jit(solution)/shard_map/ppermute | solution.py:598
  51.6 12.7 %collective-permute-start.16 = (bf16[256,512]{1,0:T(8,128)(2,1)S(1)}, bf16[256,512]{1,0:T(8,128)(2,1)S(1)}, u32[]{:S(2)}, u32[]{:S(2)}) collective-permute-start(bf16[256,512]{1,0:T(8,128)(2,1)S(1)} %get-tuple-element.34.refs_0_.kvc), channel_id=1, source_target_pairs={{0,96},{8,104},{16,112},{24,120},{32,64},{40,72},{48,80},{56,88},{... | collective-permute-start | bytes 786440 | tf_op jit(solution)/shard_map/ppermute | solution.py:565
  56.0 9.6 %collective-permute-start.15 = (bf16[256,512]{1,0:T(8,128)(2,1)S(1)}, bf16[256,512]{1,0:T(8,128)(2,1)S(1)}, u32[]{:S(2)}, u32[]{:S(2)}) collective-permute-start(bf16[256,512]{1,0:T(8,128)(2,1)S(1)} %collective-permute-done.14.refs_1_.kvb), channel_id=1, source_target_pairs={{0,96},{8,104},{16,112},{24,120},{32,64},{40,72},{48,80},{56,88},{... | collective-permute-start | bytes 786440 | tf_op jit(solution)/shard_map/ppermute | solution.py:565
  60.0 36.0 %collective-permute-start.27 = (bf16[512,512]{1,0:T(8,128)(2,1)S(1)}, bf16[512,512]{1,0:T(8,128)(2,1)S(1)}, u32[]{:S(2)}, u32[]{:S(2)}) collective-permute-start(bf16[512,512]{1,0:T(8,128)(2,1)S(1)} %get-tuple-element.43), channel_id=1, source_target_pairs={{0,24},{8,16},{16,8},{24,0},{32,56},{40,48},{48,40},{56,32},{64,88... | collective-permute-start | bytes 1572872 | tf_op jit(solution)/shard_map/ppermute | solution.py:565
  64.3 27.4 %collective-permute-start.28 = (bf16[256,512]{1,0:T(8,128)(2,1)S(1)}, bf16[256,512]{1,0:T(8,128)(2,1)S(1)}, u32[]{:S(2)}, u32[]{:S(2)}) collective-permute-start(bf16[256,512]{1,0:T(8,128)(2,1)S(1)} %get-tuple-element.39.q_ref.q), channel_id=1, source_target_pairs={{0,8},{8,0},{16,24},{24,16},{32,40},{40,32},{48,56},{56,48},{64,72... | collective-permute-start | bytes 786440 | tf_op jit(solution)/shard_map/ppermute | solution.py:565
  65.7 33.3 %collective-permute-start.17 = (bf16[512,512]{1,0:T(8,128)(2,1)S(1)}, bf16[512,512]{1,0:T(8,128)(2,1)S(1)}, u32[]{:S(2)}, u32[]{:S(2)}) collective-permute-start(bf16[512,512]{1,0:T(8,128)(2,1)S(1)} %get-tuple-element.37), channel_id=1, source_target_pairs={{0,24},{8,16},{16,8},{24,0},{32,56},{40,48},{48,40},{56,32},{64,88... | collective-permute-start | bytes 1572872 | tf_op jit(solution)/shard_map/ppermute | solution.py:565
  74.3 11.5 %collective-permute-start.36 = (bf16[64,384]{1,0:T(8,128)(2,1)S(1)}, bf16[64,384]{1,0:T(8,128)(2,1)S(1)}, u32[]{:S(2)}, u32[]{:S(2)}) collective-permute-start(bf16[64,384]{1,0:T(8,128)(2,1)S(1)} %memory_combine.10.a), channel_id=1, source_target_pairs={{0,24},{8,16},{16,8},{24,0},{32,56},{40,48},{48,40},{56,32},{64,88... | collective-permute-start | bytes 147464 | tf_op jit(solution)/shard_map/ppermute | solution.py:586
  94.6 21.1 %collective-permute-start.41 = (bf16[32,512]{1,0:T(8,128)(2,1)S(1)}, bf16[32,512]{1,0:T(8,128)(2,1)S(1)}, u32[]{:S(2)}, u32[]{:S(2)}) collective-permute-start(bf16[32,512]{1,0:T(8,128)(2,1)S(1)} %collective-permute-done.40.f), channel_id=1, source_target_pairs={{0,1},{1,0},{2,3},{3,2},{4,5},{5,4},{6,7},{7,6},{8,9},{9,8},{10,11... | collective-permute-start | bytes 98312 | tf_op jit(solution)/shard_map/ppermute | solution.py:606
  96.0 19.7 %collective-permute-start.39 = (bf16[2,32,512]{2,1,0:T(8,128)(2,1)S(1)}, bf16[2,32,512]{2,1,0:T(8,128)(2,1)S(1)}, u32[]{:S(2)}, u32[]{:S(2)}) collective-permute-start(bf16[2,32,512]{2,1,0:T(8,128)(2,1)S(1)} %collective-permute-done.38.n), channel_id=1, source_target_pairs={{0,1},{1,0},{2,3},{3,2},{4,5},{5,4},{6,7},{7,6},{8,9},{9,8},{10,11... | collective-permute-start | bytes 196616 | tf_op jit(solution)/shard_map/ppermute | solution.py:606
  97.5 7.8 %collective-permute-start.29 = (bf16[272,512]{1,0:T(8,128)(2,1)S(1)}, bf16[272,512]{1,0:T(8,128)(2,1)S(1)}, u32[]{:S(2)}, u32[]{:S(2)}) collective-permute-start(bf16[272,512]{1,0:T(8,128)(2,1)S(1)} %token_attention.7), channel_id=1, source_target_pairs={{0,8},{8,0},{16,24},{24,16},{32,40},{40,32},{48,56},{56,48},{64,72... | collective-permute-start | bytes 835592 | tf_op jit(solution)/shard_map/ppermute | solution.py:565
  100.5 10.8 %collective-permute-start.19 = (bf16[272,512]{1,0:T(8,128)(2,1)S(1)}, bf16[272,512]{1,0:T(8,128)(2,1)S(1)}, u32[]{:S(2)}, u32[]{:S(2)}) collective-permute-start(bf16[272,512]{1,0:T(8,128)(2,1)S(1)} %token_attention.5), channel_id=1, source_target_pairs={{0,8},{8,0},{16,24},{24,16},{32,40},{40,32},{48,56},{56,48},{64,72... | collective-permute-start | bytes 835592 | tf_op jit(solution)/shard_map/ppermute | solution.py:565
  113.8 8.4 %collective-permute-start.31 = (bf16[2,256,512]{2,1,0:T(8,128)(2,1)S(1)}, bf16[2,256,512]{2,1,0:T(8,128)(2,1)S(1)}, u32[]{:S(2)}, u32[]{:S(2)}) collective-permute-start(bf16[2,256,512]{2,1,0:T(8,128)(2,1)S(1)} %pair_up.6), channel_id=1, source_target_pairs={{0,2},{1,7},{2,4},{3,1},{4,6},{5,3},{6,0},{7,5},{8,10},{9,15},{10,... | collective-permute-start | bytes 1572872 | tf_op jit(solution)/shard_map/ppermute | solution.py:602
  117.7 10.7 %collective-permute-start.21 = (bf16[2,256,512]{2,1,0:T(8,128)(2,1)S(1)}, bf16[2,256,512]{2,1,0:T(8,128)(2,1)S(1)}, u32[]{:S(2)}, u32[]{:S(2)}) collective-permute-start(bf16[2,256,512]{2,1,0:T(8,128)(2,1)S(1)} %pair_up.5), channel_id=1, source_target_pairs={{0,2},{1,7},{2,4},{3,1},{4,6},{5,3},{6,0},{7,5},{8,10},{9,15},{10,... | collective-permute-start | bytes 1572872 | tf_op jit(solution)/shard_map/ppermute | solution.py:602
  122.2 14.2 %collective-permute-start.33 = (bf16[256,512]{1,0:T(8,128)(2,1)S(1)}, bf16[256,512]{1,0:T(8,128)(2,1)S(1)}, u32[]{:S(2)}, u32[]{:S(2)}) collective-permute-start(bf16[256,512]{1,0:T(8,128)(2,1)S(1)} %first_of.3), channel_id=1, source_target_pairs={{0,2},{1,7},{2,4},{3,1},{4,6},{5,3},{6,0},{7,5},{8,10},{9,15},{10,... | collective-permute-start | bytes 786440 | tf_op jit(solution)/shard_map/ppermute | solution.py:602
  125.0 9.2 %collective-permute-start.43 = (bf16[32,1792]{1,0:T(8,128)(2,1)S(1)}, bf16[32,1792]{1,0:T(8,128)(2,1)S(1)}, u32[]{:S(2)}, u32[]{:S(2)}) collective-permute-start(bf16[32,1792]{1,0:T(8,128)(2,1)S(1)} %add_convert_fusion.1), channel_id=1, source_target_pairs={{0,2},{1,3},{2,0},{3,1},{4,6},{5,7},{6,4},{7,5},{8,10},{9,11},{10,... | collective-permute-start | bytes 344072 | tf_op jit(solution)/shard_map/ppermute | solution.py:598
  125.1 10.0 %collective-permute-start.44 = (bf16[32,1792]{1,0:T(8,128)(2,1)S(1)}, bf16[32,1792]{1,0:T(8,128)(2,1)S(1)}, u32[]{:S(2)}, u32[]{:S(2)}) collective-permute-start(bf16[32,1792]{1,0:T(8,128)(2,1)S(1)} %add_convert_fusion.1), channel_id=1, source_target_pairs={{0,6},{1,7},{2,4},{3,5},{4,2},{5,3},{6,0},{7,1},{8,14},{9,15},{10,... | collective-permute-start | bytes 344072 | tf_op jit(solution)/shard_map/ppermute | solution.py:598
  125.8 10.6 %collective-permute-start.45 = (bf16[32,1792]{1,0:T(8,128)(2,1)S(1)}, bf16[32,1792]{1,0:T(8,128)(2,1)S(1)}, u32[]{:S(2)}, u32[]{:S(2)}) collective-permute-start(bf16[32,1792]{1,0:T(8,128)(2,1)S(1)} %add_convert_fusion.1), channel_id=1, source_target_pairs={{0,4},{1,5},{2,6},{3,7},{4,0},{5,1},{6,2},{7,3},{8,12},{9,13},{10,... | collective-permute-start | bytes 344072 | tf_op jit(solution)/shard_map/ppermute | solution.py:598
  128.4 10.0 %collective-permute-start.22 = (bf16[256,512]{1,0:T(8,128)(2,1)S(1)}, bf16[256,512]{1,0:T(8,128)(2,1)S(1)}, u32[]{:S(2)}, u32[]{:S(2)}) collective-permute-start(bf16[256,512]{1,0:T(8,128)(2,1)S(1)} %first_of.2), channel_id=1, source_target_pairs={{0,2},{1,7},{2,4},{3,1},{4,6},{5,3},{6,0},{7,5},{8,10},{9,15},{10,... | collective-permute-start | bytes 786440 | tf_op jit(solution)/shard_map/ppermute | solution.py:602
  134.3 7.8 %collective-permute-start.32 = (bf16[2,256,512]{2,1,0:T(8,128)(2,1)S(1)}, bf16[2,256,512]{2,1,0:T(8,128)(2,1)S(1)}, u32[]{:S(2)}, u32[]{:S(2)}) collective-permute-start(bf16[2,256,512]{2,1,0:T(8,128)(2,1)S(1)} %collective-permute-done.31.v.refs_2_), channel_id=1, source_target_pairs={{0,1},{1,0},{2,3},{3,2},{4,5},{5,4},{6,7},{7,6},{8,9},{9,8},{10,11... | collective-permute-start | bytes 1572872 | tf_op jit(solution)/shard_map/ppermute | solution.py:606
  (27 other events, 180.1 us)
